TPU v7x, 256 devices: a whole 4x4x8 slice. The times are simulated.
256 devices in a mesh: seq: 64 (over y, z, x_hi), tp: 4 (over x_lo, core).
Axes of the slice: x: 4 (x_hi: 2, x_lo: 2; x = x_hi * 2 + x_lo), y: 4, z: 8, core: 2. Of those that a mesh axis runs over, the one named last changes fastest.
Arguments:
- inputs: bfloat16 [8192, 2048], P(('seq', 'tp')), may hold values from -40 to 40
- gain: float32 [2048], replicated, may hold values from 0.5 to 1.5
- w_gate: bfloat16 [2048, 7168], P('seq', 'tp'), may hold values from -0.125 to 0.125
- w_up: bfloat16 [2048, 7168], P('seq', 'tp'), may hold values from -0.125 to 0.125
- grad_act: bfloat16 [8192, 7168], P('seq', 'tp'), may hold values from -12 to 12
Outputs:
- input_grad: bfloat16 [8192, 2048], P(('seq', 'tp'))
- gain_grad: float32 [2048], replicated
- gate_weight_grad: float32 [2048, 7168], P('seq', 'tp')
All inputs are finite; a program needn't handle non-finite values.
Results may differ from a plain program's by a relative error of at most 0.012.
Values may be sent and summed in bfloat16 or wider, within the bound.
No kernel may reach another device: no remote copies, remote signals or barrier semaphores. Data moves between devices by JAX's collectives and lax.ppermute only.
A program may use at most 128 MiB of HBM per device.

v0:
```python
import jax
import jax.numpy as jnp
from jax import lax
from jax.sharding import Mesh
from jax.sharding import PartitionSpec as P

TP = ("tp_0", "tp_1")
SEQ = ("seq_0", "seq_1", "seq_2")
SEQ_TP = ("seq_0", "seq_1", "seq_2", "tp_0", "tp_1")


def sent_to_all(value, axis):
    peers = lax.axis_size(axis)
    return lax.all_to_all(
        jnp.broadcast_to(value[None], (peers, *value.shape)), axis, 0, 0, tiled=True
    )


def laid_out(parts, dim):
    dims = list(parts.shape[1:])
    dims[dim] *= parts.shape[0]
    return jnp.moveaxis(parts, 0, dim).reshape(dims)


def collect(value, axis, dim):
    parts = sent_to_all(value, axis)
    return laid_out(parts, dim)


def in_one_piece(arrays, axis, dim, along):
    widths = [a.shape[along] for a in arrays]
    both = jnp.concatenate(arrays, axis=along)
    out = lax.all_gather(both, axis, axis=dim, tiled=True)
    return tuple(jnp.split(out, [sum(widths[:k]) for k in range(1, len(widths))], axis=along))


def split_up(value, dim, peers):
    dims = value.shape
    parts = value.reshape(*dims[:dim], peers, dims[dim] // peers, *dims[dim + 1 :])
    return jnp.moveaxis(parts, dim, 0)


def sum_at_owner(value, axis, dim):
    parts = split_up(value, dim, lax.axis_size(axis))
    arrived = lax.all_to_all(parts, axis, split_axis=0, concat_axis=0, tiled=True)
    return arrived.astype(jnp.float32).sum(axis=0)


def over_axes(value, axes):
    for axis in axes:
        value = lax.psum(value, axis)
    return value


def own_rows_2(terms, axes):
    so_far = terms.astype(jnp.bfloat16)
    for axis in axes:
        so_far = lax.psum_scatter(so_far, axis, scatter_dimension=0, tiled=True)
    return so_far.astype(jnp.float32)


def on_device(inputs, gain, w_gate, w_up, grad_act):
    group_inputs = collect(inputs, TP, 0)
    values = group_inputs.astype(jnp.float32)
    inverse = lax.rsqrt(jnp.mean(values * values, axis=-1, keepdims=True) + 1e-05)
    scaled = values * inverse
    normed = (scaled * gain).astype(jnp.bfloat16)
    full_gate, full_up = in_one_piece((w_gate, w_up), SEQ, 0, 1)
    gate = jnp.dot(normed, full_gate, preferred_element_type=jnp.float32)
    up = jnp.dot(normed, full_up, preferred_element_type=jnp.float32)
    sigmoid_gate = jax.nn.sigmoid(gate)
    cotangent = grad_act.astype(jnp.float32)
    d_up = (cotangent * gate * sigmoid_gate).astype(jnp.bfloat16)
    d_gate = (cotangent * up * sigmoid_gate * (1.0 + gate * (1.0 - sigmoid_gate))).astype(
        jnp.bfloat16
    )
    contract = (((1,), (1,)), ((), ()))
    partial_grad = lax.dot_general(d_gate, full_gate, contract, preferred_element_type=jnp.float32)
    partial_grad = partial_grad + lax.dot_general(
        d_up, full_up, contract, preferred_element_type=jnp.float32
    )
    own_grad = sum_at_owner(partial_grad.astype(jnp.bfloat16), TP, 0)
    own_rows = own_grad.shape[0]
    offset = lax.axis_index(TP) * own_rows
    own_scaled = lax.dynamic_slice_in_dim(scaled, offset, own_rows, 0)
    own_inverse = lax.dynamic_slice_in_dim(inverse, offset, own_rows, 0)
    gain_grad = over_axes(jnp.sum(own_grad * own_scaled, axis=0), SEQ_TP)
    gained = own_grad * gain
    middle = jnp.mean(gained * own_scaled, axis=-1, keepdims=True)
    input_grad = (own_inverse * (gained - own_scaled * middle)).astype(jnp.bfloat16)
    gate_weight_grad = own_rows_2(
        lax.dot_general(
            normed, d_gate, (((0,), (0,)), ((), ())), preferred_element_type=jnp.float32
        ),
        SEQ,
    )
    return (input_grad, gain_grad, gate_weight_grad)


def solution(mesh):
    torus = Mesh(mesh.devices.reshape(4, 8, 2, 2, 2), ("seq_0", "seq_1", "seq_2", "tp_0", "tp_1"))
    placed = (P(SEQ_TP, None), P(), P(SEQ, TP), P(SEQ, TP), P(SEQ, TP))
    return jax.shard_map(
        on_device,
        mesh=torus,
        in_specs=placed,
        out_specs=(P(SEQ_TP, None), P(), P(SEQ, TP)),
        check_vma=False,
    )
```

profile of v0, /device:TPU:1, one launch (start us, length us, event | category | flops | bytes accessed | tf_op | source)
XLA Modules:
  0.0 380.7 jit_solution(14655092618514983426)
XLA Ops:
  7.2 0.0 all-gather.2.cloned.1.call-start
  7.2 1.7 pad_maximum_fusion
  8.9 0.0 all-gather.2.cloned.1.call-update
  8.9 0.0 copy-start.1
  8.9 0.0 reduce-scatter.4.cloned.1.call-start
  9.0 1.0 broadcast_in_dim.2
  10.0 13.4 %all_to_all.10 = bf16[4,32,2048]{2,1,0:T(8,128)(2,1)S(1)} all-to-all(bf16[4,32,2048]{2,1,0:T(8,128)(2,1)S(1)} %broadcast_in_dim.2), channel_id=1, replica_groups=mesh['seq_0'=4,'seq_1'=8,'seq_2'=2,'tp_0'=2,'tp_1'=2] {'tp_0','tp_1'}, dimensions={0} | all-to-all | bytes 1048576 | tf_op jit(solution)/shard_map/all_to_all | solution.py:14
  23.3 0.2 multiply_reduce_fusion
  23.5 0.1 rsqrt.20
  23.6 0.9 bitcast_multiply_fusion
  24.5 184.2 %all-gather.2.cloned.1.call-done = bf16[2048,3584]{1,0:T(8,128)(2,1)} async-done(((bf16[32,3584]{1,0:T(8,128)(2,1)}), bf16[2048,3584]{1,0:T(8,128)(2,1)}) %all-gather.2.cloned.1.call-update) | async-done | bytes 14680080 | tf_op jit(solution)/shard_map/all_gather | solution.py:33
  208.7 4.2 %fusion.2 = f32[128,1792]{1,0:T(8,128)S(1)} fusion(bf16[128,2048]{1,0:T(8,128)(2,1)S(1)} %get-tuple-element.6, bf16[2048,3584]{1,0:T(8,128)(2,1)} %all-gather.2.cloned.1.call-done), kind=kOutput, calls=%fused_computation.3 | convolution fusion | flops 939524096 | bytes 8781824 | tf_op jit(solution)/shard_map/dot_general | solution.py:69
  212.9 0.0 copy-done.1
  212.9 4.5 %fusion.23 = bf16[128,1792]{1,0:T(8,128)(2,1)S(1)} fusion(bf16[128,2048]{1,0:T(8,128)(2,1)S(1)} %get-tuple-element.6, bf16[2048,3584]{1,0:T(8,128)(2,1)} %all-gather.2.cloned.1.call-done, bf16[128,1792]{1,0:T(8,128)(2,1)S(1)} %copy-done.1, f32[128,1792]{1,0:T(8,128)S(1)} %fusion.2), kind=kOutput, calls=%fused_computation.14 | convolution fusion | flops 942047232 | bytes 9699328 | tf_op jit(solution)/shard_map/dot_general | solution.py:70
  217.4 5.0 %convolution_convert_fusion = bf16[2048,1792]{1,0:T(8,128)(2,1)} fusion(bf16[128,2048]{1,0:T(8,128)(2,1)S(1)} %get-tuple-element.6, bf16[128,1792]{1,0:T(8,128)(2,1)S(1)} %fusion.23), kind=kOutput, calls=%fused_computation | convolution fusion | flops 943194112 | bytes 8323072 | tf_op jit(solution)/shard_map/dot_general | solution.py:92
  222.5 0.0 reduce-scatter.4.cloned.1.call-update
  222.5 0.0 reduce-scatter.6.cloned.1.call-start
  222.5 72.7 %reduce-scatter.4.cloned.1.call-done = bf16[512,1792]{1,0:T(8,128)(2,1)} async-done(((bf16[2048,1792]{1,0:T(8,128)(2,1)}), bf16[512,1792]{1,0:T(8,128)(2,1)}) %reduce-scatter.4.cloned.1.call-update) | async-done | bytes 1835024 | tf_op jit(solution)/shard_map/reduce_scatter | solution.py:58
  295.2 0.0 reduce-scatter.6.cloned.1.call-update
  295.3 5.5 %fusion = f32[128,2048]{1,0:T(8,128)S(1)} fusion(bf16[128,1792]{1,0:T(8,128)(2,1)S(1)} %fusion.23, bf16[2048,3584]{1,0:T(8,128)(2,1)} %all-gather.2.cloned.1.call-done), kind=kOutput, calls=%fused_computation.1 | convolution fusion | flops 939524096 | bytes 8847360 | tf_op jit(solution)/shard_map/dot_general | solution.py:78
  300.8 0.0 copy-start
  300.8 6.4 %fusion.20 = bf16[128,2048]{1,0:T(8,128)(2,1)} fusion(f32[128,2048]{1,0:T(8,128)S(1)} %fusion, bf16[2048,3584]{1,0:T(8,128)(2,1)} %all-gather.2.cloned.1.call-done, f32[128,1792]{1,0:T(8,128)S(1)} %fusion.2, bf16[128,1792]{1,0:T(8,128)(2,1)S(1)} %copy-done.1), kind=kOutput, calls=%fused_computation.13 | convolution fusion | flops 941654016 | bytes 10289152 | tf_op jit(solution)/shard_map/dot_general | solution.py:79
  307.2 4.2 %all-to-all-start.1 = ((bf16[4,32,2048]{2,1,0:T(8,128)(2,1)}), bf16[4,32,2048]{2,1,0:T(8,128)(2,1)S(1)}, u32[]{:S(2)}, u32[]{:S(2)}) async-start(bf16[4,32,2048]{2,1,0:T(8,128)(2,1)} %bitcast.2), calls=%async_computation.1 | async-start | bytes 1048576 | tf_op jit(solution)/shard_map/all_to_all | solution.py:45
  311.4 0.0 reduce-scatter.8.cloned.1.call-start
  311.4 0.1 rsqrt.19
  311.5 0.1 dynamic-slice_bitcast_fusion
  311.5 7.7 %all-to-all-done.1 = bf16[4,32,2048]{2,1,0:T(8,128)(2,1)S(1)} async-done(((bf16[4,32,2048]{2,1,0:T(8,128)(2,1)}), bf16[4,32,2048]{2,1,0:T(8,128)(2,1)S(1)}, u32[]{:S(2)}, u32[]{:S(2)}) %all-to-all-start.1) | async-done | bytes 524320 | tf_op jit(solution)/shard_map/all_to_all | solution.py:45
  319.2 0.1 convert_reduce_fusion
  319.3 0.0 copy-done
  319.3 0.2 multiply_reduce_fusion.1
  319.5 7.5 %psum.35 = f32[2048]{0:T(1024)S(1)} all-reduce(f32[2048]{0:T(1024)S(1)} %get-tuple-element.3), channel_id=1, replica_groups=mesh['seq_0'=4,'seq_1'=8,'seq_2'=2,'tp_0'=2,'tp_1'=2] {'seq_0'}, use_global_device_ids=true, to_apply=%region_4.0 | all-reduce | flops 2048 | bytes 16384 | tf_op jit(solution)/shard_map/psum | solution.py:51
  327.0 13.8 %psum.36 = f32[2048]{0:T(1024)S(1)} all-reduce(f32[2048]{0:T(1024)S(1)} %psum.35), channel_id=1, replica_groups=mesh['seq_0'=4,'seq_1'=8,'seq_2'=2,'tp_0'=2,'tp_1'=2] {'seq_1'}, use_global_device_ids=true, to_apply=%region_5.0 | all-reduce | flops 2048 | bytes 16384 | tf_op jit(solution)/shard_map/psum | solution.py:51
  340.8 5.4 %psum.37 = f32[2048]{0:T(1024)S(1)} all-reduce(f32[2048]{0:T(1024)S(1)} %psum.36), channel_id=1, replica_groups=mesh['seq_0'=4,'seq_1'=8,'seq_2'=2,'tp_0'=2,'tp_1'=2] {'seq_2'}, use_global_device_ids=true, to_apply=%region_6.0 | all-reduce | flops 2048 | bytes 16384 | tf_op jit(solution)/shard_map/psum | solution.py:51
  346.2 3.8 %psum.38 = f32[2048]{0:T(1024)S(1)} all-reduce(f32[2048]{0:T(1024)S(1)} %psum.37), channel_id=1, replica_groups=mesh['seq_0'=4,'seq_1'=8,'seq_2'=2,'tp_0'=2,'tp_1'=2] {'tp_0'}, use_global_device_ids=true, to_apply=%region_7.0 | all-reduce | flops 2048 | bytes 16384 | tf_op jit(solution)/shard_map/psum | solution.py:51
  350.0 0.0 reduce-scatter.6.cloned.1.call-done
  350.1 0.0 reduce-scatter.8.cloned.1.call-update
  350.1 11.1 %psum.39 = f32[2048]{0:T(1024)} all-reduce(f32[2048]{0:T(1024)S(1)} %psum.38), channel_id=1, replica_groups=mesh['seq_0'=4,'seq_1'=8,'seq_2'=2,'tp_0'=2,'tp_1'=2] {'tp_1'}, use_global_device_ids=true, to_apply=%region_8.0 | all-reduce | flops 2048 | bytes 16384 | tf_op jit(solution)/shard_map/psum | solution.py:51
  361.1 0.8 multiply_convert_fusion.1
  361.9 10.7 %reduce-scatter.8.cloned.1.call-done = bf16[32,1792]{1,0:T(8,128)(2,1)} async-done(((bf16[64,1792]{1,0:T(8,128)(2,1)}), bf16[32,1792]{1,0:T(8,128)(2,1)}) %reduce-scatter.8.cloned.1.call-update) | async-done | bytes 114704 | tf_op jit(solution)/shard_map/reduce_scatter | solution.py:58
  372.6 1.6 convert_element_type.47
  (2 shorter events, 0.0 us)
Async XLA Ops:
  7.2 201.5 %all-gather.2.cloned.1.call-start = ((), (), s32[]{:S(2)}) async-start(), calls=%async_computation.5 | async-start | bytes 14909440 | tf_op jit(solution)/shard_map/all_gather | solution.py:33
  8.9 204.0 %copy-start.1 = (bf16[128,1792]{1,0:T(8,128)(2,1)S(1)}, bf16[128,1792]{1,0:T(8,128)(2,1)}, u32[]{:S(2)}) copy-start(bf16[128,1792]{1,0:T(8,128)(2,1)} %param.9) | copy-start | bytes 1376260
  8.9 286.3 %reduce-scatter.4.cloned.1.call-start = ((), (), s32[]{:S(2)}) async-start(), calls=%async_computation.6 | async-start | bytes 9175040 | tf_op jit(solution)/shard_map/reduce_scatter | solution.py:58
  222.5 127.6 %reduce-scatter.6.cloned.1.call-start = ((), (), s32[]{:S(2)}) async-start(), calls=%async_computation.7 | async-start | bytes 2064384 | tf_op jit(solution)/shard_map/reduce_scatter | solution.py:58
  300.8 18.5 %copy-start = (f32[2048]{0:T(1024)S(1)}, f32[2048]{0:T(1024)}, u32[]{:S(2)}) copy-start(f32[2048]{0:T(1024)} %param.6) | copy-start | bytes 24580
  307.2 12.0 %all-to-all-start.1 = ((bf16[4,32,2048]{2,1,0:T(8,128)(2,1)}), bf16[4,32,2048]{2,1,0:T(8,128)(2,1)S(1)}, u32[]{:S(2)}, u32[]{:S(2)}) async-start(bf16[4,32,2048]{2,1,0:T(8,128)(2,1)} %bitcast.2), calls=%async_computation.1 | async-start | bytes 1048576 | tf_op jit(solution)/shard_map/all_to_all | solution.py:45
  311.4 61.2 %reduce-scatter.8.cloned.1.call-start = ((), (), s32[]{:S(2)}) async-start(), calls=%async_computation.8 | async-start | bytes 344064 | tf_op jit(solution)/shard_map/reduce_scatter | solution.py:58
Sparse Core Ops, SparseCore 0:
  12.2 196.4 all-gather.1
  222.6 72.5 reduce-scatter.3
  297.8 37.3 reduce-scatter.5
  350.2 22.3 reduce-scatter.7
where the time goes:
time: 381 us
  waiting for transfers between devices  275 us (72%)
  blocking collectives  55 us (14%)
  matrix products  25.7 us (7%)
  between operations  13.9 us (4%)
  other arithmetic  5.36 us (1%)
  starting transfers between devices  4.29 us (1%)
    all_gather x1, waiting for transfers between devices, in_one_piece(): out = lax.all_gather(both, axis, axis=dim, tiled=True)  184 us
    reduce_scatter x3, waiting for transfers between devices, own_rows_2(): so_far = lax.psum_scatter(so_far, axis, scatter_dimension=0, tiled=True)  83.4 us
    psum x5, blocking collectives, over_axes(): value = lax.psum(value, axis)  41.6 us
    all_to_all x1, blocking collectives, sent_to_all(): lax.all_to_all(jnp.broadcast_to(value[None], (peers, *value.shape)), axis...  13.4 us
    all_to_all x1, waiting for transfers between devices, sum_at_owner(): lax.all_to_all(parts, axis, split_axis=0, concat_axis=0, tiled=True)  7.69 us
  transfers between devices with their start and end apart: 5, of which 4 were waited for; matrix products, arithmetic and copies ran while one was open for 4% of the time, Pallas kernels for 0%

commit v1 on v0

--- a/solution.py
+++ b/solution.py
@@ -48,7 +48,7 @@
 
 def over_axes(value, axes):
     for axis in axes:
-        value = lax.psum(value, axis)
+        value = jnp.sum(lax.all_gather(value, axis), axis=0)
     return value
 
 

time: 381 us -> 393 us (1.031)
  blocking collectives: 55 us -> 64 us
    all_gather x0 -> x5, blocking collectives: none -> 50.6 us  [over_axes(): value = jnp.sum(lax.all_gather(value, axis), axis=0)]
    psum x5 -> x0, blocking collectives: 41.6 us -> none  [over_axes(): value = lax.psum(value, axis)]
where the time goes in v1:
time: 393 us
  waiting for transfers between devices  277 us (70%)
  blocking collectives  64 us (16%)
  matrix products  25.7 us (7%)
  between operations  13.9 us (4%)
  other arithmetic  6.07 us (2%)
  starting transfers between devices  4.29 us (1%)
    all_gather x1, waiting for transfers between devices, in_one_piece(): out = lax.all_gather(both, axis, axis=dim, tiled=True)  184 us
    reduce_scatter x3, waiting for transfers between devices, own_rows_2(): so_far = lax.psum_scatter(so_far, axis, scatter_dimension=0, tiled=True)  85.4 us
    all_gather x5, blocking collectives, over_axes(): value = jnp.sum(lax.all_gather(value, axis), axis=0)  50.6 us
    all_to_all x1, blocking collectives, sent_to_all(): lax.all_to_all(jnp.broadcast_to(value[None], (peers, *value.shape)), axis...  13.4 us
  transfers between devices with their start and end apart: 5, of which 4 were waited for; matrix products, arithmetic and copies ran while one was open for 4% of the time, Pallas kernels for 0%

profile of v1, /device:TPU:1, one launch (start us, length us, event | category | flops | bytes accessed | tf_op | source)
XLA Modules:
  0.0 392.6 jit_solution(2913457596314140396)
XLA Ops:
  7.2 0.0 all-gather.7.cloned.1.call-start
  7.2 1.7 pad_maximum_fusion
  8.9 0.0 all-gather.7.cloned.1.call-update
  8.9 0.0 copy-start.1
  8.9 0.0 reduce-scatter.4.cloned.1.call-start
  9.0 1.0 broadcast_in_dim.2
  10.0 13.4 %all_to_all.10 = bf16[4,32,2048]{2,1,0:T(8,128)(2,1)S(1)} all-to-all(bf16[4,32,2048]{2,1,0:T(8,128)(2,1)S(1)} %broadcast_in_dim.2), channel_id=1, replica_groups=mesh['seq_0'=4,'seq_1'=8,'seq_2'=2,'tp_0'=2,'tp_1'=2] {'tp_0','tp_1'}, dimensions={0} | all-to-all | bytes 1048576 | tf_op jit(solution)/shard_map/all_to_all | solution.py:14
  23.3 0.2 multiply_reduce_fusion
  23.5 0.1 rsqrt.20
  23.6 0.9 bitcast_multiply_fusion
  24.5 184.2 %all-gather.7.cloned.1.call-done = bf16[2048,3584]{1,0:T(8,128)(2,1)} async-done(((bf16[32,3584]{1,0:T(8,128)(2,1)}), bf16[2048,3584]{1,0:T(8,128)(2,1)}) %all-gather.7.cloned.1.call-update) | async-done | bytes 14680080 | tf_op jit(solution)/shard_map/all_gather | solution.py:33
  208.7 4.2 %fusion.2 = f32[128,1792]{1,0:T(8,128)S(1)} fusion(bf16[128,2048]{1,0:T(8,128)(2,1)S(1)} %get-tuple-element.6, bf16[2048,3584]{1,0:T(8,128)(2,1)} %all-gather.7.cloned.1.call-done), kind=kOutput, calls=%fused_computation.3 | convolution fusion | flops 939524096 | bytes 8781824 | tf_op jit(solution)/shard_map/dot_general | solution.py:69
  212.9 0.0 copy-done.1
  212.9 4.5 %fusion.23 = bf16[128,1792]{1,0:T(8,128)(2,1)S(1)} fusion(bf16[128,2048]{1,0:T(8,128)(2,1)S(1)} %get-tuple-element.6, bf16[2048,3584]{1,0:T(8,128)(2,1)} %all-gather.7.cloned.1.call-done, bf16[128,1792]{1,0:T(8,128)(2,1)S(1)} %copy-done.1, f32[128,1792]{1,0:T(8,128)S(1)} %fusion.2), kind=kOutput, calls=%fused_computation.14 | convolution fusion | flops 942047232 | bytes 9699328 | tf_op jit(solution)/shard_map/dot_general | solution.py:70
  217.4 5.0 %convolution_convert_fusion = bf16[2048,1792]{1,0:T(8,128)(2,1)} fusion(bf16[128,2048]{1,0:T(8,128)(2,1)S(1)} %get-tuple-element.6, bf16[128,1792]{1,0:T(8,128)(2,1)S(1)} %fusion.23), kind=kOutput, calls=%fused_computation | convolution fusion | flops 943194112 | bytes 8323072 | tf_op jit(solution)/shard_map/dot_general | solution.py:92
  222.5 0.0 reduce-scatter.4.cloned.1.call-update
  222.5 0.0 reduce-scatter.6.cloned.1.call-start
  222.5 72.7 %reduce-scatter.4.cloned.1.call-done = bf16[512,1792]{1,0:T(8,128)(2,1)} async-done(((bf16[2048,1792]{1,0:T(8,128)(2,1)}), bf16[512,1792]{1,0:T(8,128)(2,1)}) %reduce-scatter.4.cloned.1.call-update) | async-done | bytes 1835024 | tf_op jit(solution)/shard_map/reduce_scatter | solution.py:58
  295.2 0.0 reduce-scatter.6.cloned.1.call-update
  295.3 5.5 %fusion = f32[128,2048]{1,0:T(8,128)S(1)} fusion(bf16[128,1792]{1,0:T(8,128)(2,1)S(1)} %fusion.23, bf16[2048,3584]{1,0:T(8,128)(2,1)} %all-gather.7.cloned.1.call-done), kind=kOutput, calls=%fused_computation.1 | convolution fusion | flops 939524096 | bytes 8847360 | tf_op jit(solution)/shard_map/dot_general | solution.py:78
  300.8 0.0 copy-start
  300.8 6.4 %fusion.20 = bf16[128,2048]{1,0:T(8,128)(2,1)} fusion(f32[128,2048]{1,0:T(8,128)S(1)} %fusion, bf16[2048,3584]{1,0:T(8,128)(2,1)} %all-gather.7.cloned.1.call-done, f32[128,1792]{1,0:T(8,128)S(1)} %fusion.2, bf16[128,1792]{1,0:T(8,128)(2,1)S(1)} %copy-done.1), kind=kOutput, calls=%fused_computation.13 | convolution fusion | flops 941654016 | bytes 10289152 | tf_op jit(solution)/shard_map/dot_general | solution.py:79
  307.2 4.2 %all-to-all-start.1 = ((bf16[4,32,2048]{2,1,0:T(8,128)(2,1)}), bf16[4,32,2048]{2,1,0:T(8,128)(2,1)S(1)}, u32[]{:S(2)}, u32[]{:S(2)}) async-start(bf16[4,32,2048]{2,1,0:T(8,128)(2,1)} %bitcast.2), calls=%async_computation.1 | async-start | bytes 1048576 | tf_op jit(solution)/shard_map/all_to_all | solution.py:45
  311.4 0.0 reduce-scatter.8.cloned.1.call-start
  311.4 0.1 rsqrt.19
  311.5 0.1 dynamic-slice_bitcast_fusion
  311.5 7.7 %all-to-all-done.1 = bf16[4,32,2048]{2,1,0:T(8,128)(2,1)S(1)} async-done(((bf16[4,32,2048]{2,1,0:T(8,128)(2,1)}), bf16[4,32,2048]{2,1,0:T(8,128)(2,1)S(1)}, u32[]{:S(2)}, u32[]{:S(2)}) %all-to-all-start.1) | async-done | bytes 524320 | tf_op jit(solution)/shard_map/all_to_all | solution.py:45
  319.2 0.1 convert_reduce_fusion
  319.3 0.0 copy-done
  319.3 0.2 multiply_reduce_fusion.1
  319.5 9.7 %all-gather = f32[8192]{0:T(1024)S(1)} all-gather(f32[2048]{0:T(1024)S(1)} %get-tuple-element.3), channel_id=2, replica_groups=mesh['seq_0'=4,'seq_1'=8,'seq_2'=2,'tp_0'=2,'tp_1'=2] {'seq_0'}, dimensions={0}, use_global_device_ids=true | all-gather | bytes 40960 | tf_op jit(solution)/shard_map/all_gather | solution.py:51
  329.3 20.3 %all-gather.1 = f32[16384]{0:T(1024)S(1)} all-gather(f32[2048]{0:T(1024)S(1)} %reduce_sum.85), channel_id=3, replica_groups=mesh['seq_0'=4,'seq_1'=8,'seq_2'=2,'tp_0'=2,'tp_1'=2] {'seq_1'}, dimensions={0}, use_global_device_ids=true | all-gather | bytes 73728 | tf_op jit(solution)/shard_map/all_gather | solution.py:51
  349.6 4.7 %all-gather.2 = f32[4096]{0:T(1024)S(1)} all-gather(f32[2048]{0:T(1024)S(1)} %reduce_sum.86), channel_id=4, replica_groups=mesh['seq_0'=4,'seq_1'=8,'seq_2'=2,'tp_0'=2,'tp_1'=2] {'seq_2'}, dimensions={0}, use_global_device_ids=true | all-gather | bytes 24576 | tf_op jit(solution)/shard_map/all_gather | solution.py:51
  354.4 3.5 all-gather.3
  357.9 0.0 reduce-scatter.6.cloned.1.call-done
  357.9 0.0 reduce-scatter.8.cloned.1.call-update
  357.9 12.4 %all-gather.4 = f32[4096]{0:T(1024)S(1)} all-gather(f32[2048]{0:T(1024)S(1)} %reduce_sum.88), channel_id=6, replica_groups=mesh['seq_0'=4,'seq_1'=8,'seq_2'=2,'tp_0'=2,'tp_1'=2] {'tp_1'}, dimensions={0}, use_global_device_ids=true | all-gather | bytes 24576 | tf_op jit(solution)/shard_map/all_gather | solution.py:51
  370.4 0.6 reduce_sum.89
  371.0 0.8 multiply_convert_fusion.1
  371.7 12.7 %reduce-scatter.8.cloned.1.call-done = bf16[32,1792]{1,0:T(8,128)(2,1)} async-done(((bf16[64,1792]{1,0:T(8,128)(2,1)}), bf16[32,1792]{1,0:T(8,128)(2,1)}) %reduce-scatter.8.cloned.1.call-update) | async-done | bytes 114704 | tf_op jit(solution)/shard_map/reduce_scatter | solution.py:58
  384.4 1.6 convert_element_type.47
  (11 shorter events, 0.2 us)
Async XLA Ops:
  7.2 201.5 %all-gather.7.cloned.1.call-start = ((), (), s32[]{:S(2)}) async-start(), calls=%async_computation.5 | async-start | bytes 14909440 | tf_op jit(solution)/shard_map/all_gather | solution.py:33
  8.9 204.0 %copy-start.1 = (bf16[128,1792]{1,0:T(8,128)(2,1)S(1)}, bf16[128,1792]{1,0:T(8,128)(2,1)}, u32[]{:S(2)}) copy-start(bf16[128,1792]{1,0:T(8,128)(2,1)} %param.9) | copy-start | bytes 1376260
  8.9 286.3 %reduce-scatter.4.cloned.1.call-start = ((), (), s32[]{:S(2)}) async-start(), calls=%async_computation.6 | async-start | bytes 9175040 | tf_op jit(solution)/shard_map/reduce_scatter | solution.py:58
  222.5 135.4 %reduce-scatter.6.cloned.1.call-start = ((), (), s32[]{:S(2)}) async-start(), calls=%async_computation.7 | async-start | bytes 2064384 | tf_op jit(solution)/shard_map/reduce_scatter | solution.py:58
  300.8 18.5 %copy-start = (f32[2048]{0:T(1024)S(1)}, f32[2048]{0:T(1024)}, u32[]{:S(2)}) copy-start(f32[2048]{0:T(1024)} %param.6) | copy-start | bytes 24580
  307.2 12.0 %all-to-all-start.1 = ((bf16[4,32,2048]{2,1,0:T(8,128)(2,1)}), bf16[4,32,2048]{2,1,0:T(8,128)(2,1)S(1)}, u32[]{:S(2)}, u32[]{:S(2)}) async-start(bf16[4,32,2048]{2,1,0:T(8,128)(2,1)} %bitcast.2), calls=%async_computation.1 | async-start | bytes 1048576 | tf_op jit(solution)/shard_map/all_to_all | solution.py:45
  311.4 73.1 %reduce-scatter.8.cloned.1.call-start = ((), (), s32[]{:S(2)}) async-start(), calls=%async_computation.8 | async-start | bytes 344064 | tf_op jit(solution)/shard_map/reduce_scatter | solution.py:58
Sparse Core Ops, SparseCore 0:
  12.2 196.4 all-gather.6
  222.6 72.5 reduce-scatter.3
  297.8 37.3 reduce-scatter.5
  358.0 26.3 reduce-scatter.7
